TPU v7x, 32 devices: a whole 2x2x4 slice. The times are simulated.
32 devices in a mesh: rows: 8 (over y, x, core), cols: 4 (over z).
Axes of the slice: x: 2, y: 2, z: 4, core: 2. Of those that a mesh axis runs over, the one named last changes fastest.
Arguments:
- one_query: float32 [8192, 8192], P('rows', 'cols'), may hold values from -0.09375 to 0.09375
- other_query: float32 [8192, 8192], P('rows', 'cols'), may hold values from -0.0625 to 0.0625
- one_key: float32 [8192, 512], P('rows', 'cols'), may hold values from -0.09375 to 0.09375
- other_key: float32 [8192, 512], P('rows', 'cols'), may hold values from -0.0625 to 0.0625
- one_value: float32 [8192, 512], P('rows', 'cols'), may hold values from -0.09375 to 0.09375
- other_value: float32 [8192, 512], P('rows', 'cols'), may hold values from -0.0625 to 0.0625
- mix_share: float32 [8192], P('rows'), may hold values from 0.2 to 0.8
- norm_gain: float32 [8192], P('rows'), may hold values from 0.25 to 1.75
Outputs:
- serve_query: bfloat16 [8192, 8192], P(None, 'cols')
- serve_key: bfloat16 [8192, 512], P(None, 'cols')
- serve_value: bfloat16 [8192, 512], P(None, 'cols')
- scale_query: float32 [8192], P('cols')
- scale_key: float32 [512], P('cols')
- scale_value: float32 [512], P('cols')
All inputs are finite; a program needn't handle non-finite values. Where the computation divides by a largest or mean magnitude, that divisor is 1e-20 or more.
Results may differ from a plain program's by a relative error of at most 0.001.
Values may be sent and summed in bfloat16 or wider, within the bound.
A program may use at most 192 MiB of HBM per device.

v0:
```python
import jax
import jax.numpy as jnp
from jax import lax
from jax.sharding import PartitionSpec as P

D_MODEL = 8192


def local(one_query, other_query, one_key, other_key, one_value, other_value, mix_share, norm_gain):
    fresh_query = mix_share[:, None] * one_query + (1.0 - mix_share[:, None]) * other_query
    fresh_key = mix_share[:, None] * one_key + (1.0 - mix_share[:, None]) * other_key
    fresh_value = mix_share[:, None] * one_value + (1.0 - mix_share[:, None]) * other_value
    fresh_gained_query = fresh_query * norm_gain[:, None]
    fresh_gained_key = fresh_key * norm_gain[:, None]
    fresh_gained_value = fresh_value * norm_gain[:, None]
    total_query, total_key, total_value = lax.psum(
        (
            jnp.sum(jnp.abs(fresh_gained_query), axis=0),
            jnp.sum(jnp.abs(fresh_gained_key), axis=0),
            jnp.sum(jnp.abs(fresh_gained_value), axis=0),
        ),
        "rows",
    )
    scale_query = total_query / D_MODEL
    scale_key = total_key / D_MODEL
    scale_value = total_value / D_MODEL
    narrow_query, narrow_key, narrow_value = (
        (fresh_gained_query / scale_query).astype(jnp.bfloat16),
        (fresh_gained_key / scale_key).astype(jnp.bfloat16),
        (fresh_gained_value / scale_value).astype(jnp.bfloat16),
    )
    serve_query, serve_key, serve_value = (
        lax.all_gather(narrow_query, "rows", axis=0, tiled=True),
        lax.all_gather(narrow_key, "rows", axis=0, tiled=True),
        lax.all_gather(narrow_value, "rows", axis=0, tiled=True),
    )
    return (serve_query, serve_key, serve_value, scale_query, scale_key, scale_value)


def solution(mesh):
    return jax.shard_map(
        local,
        mesh=mesh,
        in_specs=(
            P("rows", "cols"),
            P("rows", "cols"),
            P("rows", "cols"),
            P("rows", "cols"),
            P("rows", "cols"),
            P("rows", "cols"),
            P("rows"),
            P("rows"),
        ),
        out_specs=(
            P(None, "cols"),
            P(None, "cols"),
            P(None, "cols"),
            P("cols"),
            P("cols"),
            P("cols"),
        ),
        check_vma=False,
    )
```

profile of v0, /device:TPU:0, one launch (start us, length us, event | category | flops | bytes accessed | tf_op | source)
XLA Modules:
  0.0 289.0 jit_solution(13169696335159695378)
XLA Ops:
  7.2 0.0 all-gather.6.cloned.1.call-start
  7.2 0.7 broadcast_subtract_fusion
  7.9 0.0 copy-start.5
  7.9 0.0 copy-start.7
  7.9 10.0 %abs_reduce_fusion = (f32[2048]{0:T(1024)S(1)}, f32[1024,2048]{1,0:T(8,128)}) fusion(f32[1024]{0:T(1024)} %param.15, f32[1024,2048]{1,0:T(8,128)} %param.9, f32[1024]{0:T(1024)S(1)} %broadcast_subtract_fusion, f32[1024,2048]{1,0:T(8,128)} %param.8, f32[1024]{0:T(1024)} %param.14), kind=kLoop, calls=%fused_computation.1 | loop fusion | flops 12580864 | bytes 25186304 | tf_op jit(solution)/shard_map/reduce_sum | solution.py:18
  18.0 0.5 abs_reduce_fusion.1
  18.5 15.7 %all-reduce = (f32[2048]{0:T(1024)S(1)}, f32[128]{0:T(128)S(1)}, f32[128]{0:T(128)S(1)}) all-reduce(f32[2048]{0:T(1024)S(1)} %get-tuple-element.13, f32[128]{0:T(128)S(1)} %get-tuple-element.15, f32[128]{0:T(128)S(1)} %get-tuple-element.9), channel_id=1, replica_groups=mesh['rows'=8,'cols'=4] {'rows'}, use_global_device_ids=true, to_apply=%region_1.0 | all-reduce | flops 2304 | bytes 18432 | tf_op jit(solution)/shard_map/psum | solution.py:16
  34.2 0.0 copy-start.8
  34.2 0.8 divide_convert_fusion.2
  35.0 0.0 all-gather.6.cloned.1.call-update
  35.0 0.0 all-gather.8.cloned.1.call-start
  35.1 0.0 copy-start.9
  35.1 0.8 divide_convert_fusion.1
  35.9 0.0 all-gather.8.cloned.1.call-update
  35.9 0.0 all-gather.4.cloned.1.call-start
  35.9 0.0 copy-start.6
  35.9 6.6 %divide_convert_fusion = bf16[1024,2048]{1,0:T(8,128)(2,1)} fusion(f32[1024,2048]{1,0:T(8,128)} %get-tuple-element.14, f32[2048]{0:T(1024)S(1)} %broadcast_multiply_fusion), kind=kLoop, calls=%fused_computation | loop fusion | flops 4194304 | bytes 12591104 | tf_op jit(solution)/shard_map/convert_element_type | solution.py:28
  42.6 0.0 all-gather.4.cloned.1.call-update
  42.6 19.7 %all-gather.6.cloned.1.call-done = bf16[8192,128]{1,0:T(8,128)(2,1)} async-done(((bf16[1024,128]{1,0:T(8,128)(2,1)}), bf16[8192,128]{1,0:T(8,128)(2,1)}) %all-gather.6.cloned.1.call-update) | async-done | bytes 2097168 | tf_op jit(solution)/shard_map/all_gather | solution.py:34
  62.3 30.3 %all-gather.8.cloned.1.call-done = bf16[8192,128]{1,0:T(8,128)(2,1)} async-done(((bf16[1024,128]{1,0:T(8,128)(2,1)}), bf16[8192,128]{1,0:T(8,128)(2,1)}) %all-gather.8.cloned.1.call-update) | async-done | bytes 2097168 | tf_op jit(solution)/shard_map/all_gather | solution.py:35
  92.6 162.6 %all-gather.4.cloned.1.call-done = bf16[8192,2048]{1,0:T(8,128)(2,1)} async-done(((bf16[1024,2048]{1,0:T(8,128)(2,1)}), bf16[8192,2048]{1,0:T(8,128)(2,1)}) %all-gather.4.cloned.1.call-update) | async-done | bytes 33554448 | tf_op jit(solution)/shard_map/all_gather | solution.py:33
  255.2 22.9 %copy.17 = bf16[8192,2048]{1,0:T(8,128)(2,1)} copy(bf16[8192,2048]{1,0:T(8,128)(2,1)} %all-gather.4.cloned.1.call-done) | data formatting | bytes 67108864
  278.1 1.3 copy.18
  279.4 3.0 %copy.19 = bf16[8192,128]{1,0:T(8,128)(2,1)} copy(bf16[8192,128]{1,0:T(8,128)(2,1)} %all-gather.8.cloned.1.call-done) | data formatting | bytes 4194304
  (18 shorter events, 0.0 us)
Async XLA Ops:
  7.2 55.2 %all-gather.6.cloned.1.call-start = ((), (), s32[]{:S(2)}) async-start(), calls=%async_computation.1 | async-start | bytes 2359296 | tf_op jit(solution)/shard_map/all_gather | solution.py:34
  7.9 10.1 %copy-start.1 = (f32[1024,128]{1,0:T(8,128)S(1)}, f32[1024,128]{1,0:T(8,128)}, u32[]{:S(2)}) copy-start(f32[1024,128]{1,0:T(8,128)} %param.13) | copy-start | bytes 1572868
  7.9 10.1 %copy-start.2 = (f32[1024,128]{1,0:T(8,128)S(1)}, f32[1024,128]{1,0:T(8,128)}, u32[]{:S(2)}) copy-start(f32[1024,128]{1,0:T(8,128)} %param.12) | copy-start | bytes 1572868
  7.9 10.1 %copy-start.3 = (f32[1024,128]{1,0:T(8,128)S(1)}, f32[1024,128]{1,0:T(8,128)}, u32[]{:S(2)}) copy-start(f32[1024,128]{1,0:T(8,128)} %param.11) | copy-start | bytes 1572868
  7.9 10.1 %copy-start.4 = (f32[1024,128]{1,0:T(8,128)S(1)}, f32[1024,128]{1,0:T(8,128)}, u32[]{:S(2)}) copy-start(f32[1024,128]{1,0:T(8,128)} %param.10) | copy-start | bytes 1572868
  7.9 10.1 %copy-start.5 = (f32[1024]{0:T(1024)S(1)}, f32[1024]{0:T(1024)}, u32[]{:S(2)}) copy-start(f32[1024]{0:T(1024)} %param.14) | copy-start | bytes 12292
  7.9 10.1 %copy-start.7 = (f32[1024]{0:T(1024)S(1)}, f32[1024]{0:T(1024)}, u32[]{:S(2)}) copy-start(f32[1024]{0:T(1024)} %param.15) | copy-start | bytes 12292
  34.2 8.4 %copy-start.8 = (f32[128]{0:T(128)}, f32[128]{0:T(128)S(1)}, u32[]{:S(2)}) copy-start(f32[128]{0:T(128)S(1)} %broadcast_multiply_fusion.2) | copy-start | bytes 1540
  35.0 57.6 %all-gather.8.cloned.1.call-start = ((), (), s32[]{:S(2)}) async-start(), calls=%async_computation.2 | async-start | bytes 2359296 | tf_op jit(solution)/shard_map/all_gather | solution.py:35
  35.1 7.5 %copy-start.9 = (f32[128]{0:T(128)}, f32[128]{0:T(128)S(1)}, u32[]{:S(2)}) copy-start(f32[128]{0:T(128)S(1)} %broadcast_multiply_fusion.1) | copy-start | bytes 1540
  35.9 219.3 %all-gather.4.cloned.1.call-start = ((), (), s32[]{:S(2)}) async-start(), calls=%async_computation | async-start | bytes 37748736 | tf_op jit(solution)/shard_map/all_gather | solution.py:33
  35.9 6.7 %copy-start.6 = (f32[2048]{0:T(1024)}, f32[2048]{0:T(1024)S(1)}, u32[]{:S(2)}) copy-start(f32[2048]{0:T(1024)S(1)} %broadcast_multiply_fusion) | copy-start | bytes 24580
  62.3 215.7 %copy-start = (bf16[8192,128]{1,0:T(8,128)(2,1)S(1)}, bf16[8192,128]{1,0:T(8,128)(2,1)}, u32[]{:S(2)}) copy-start(bf16[8192,128]{1,0:T(8,128)(2,1)} %all-gather.6.cloned.1.call-done) | copy-start | bytes 6291460
Sparse Core Ops, SparseCore 0:
  35.1 27.1 all-gather.5
  64.8 27.7 all-gather.7
  94.5 160.6 all-gather.3
where the time goes:
time: 289 us
  waiting for transfers between devices  213 us (74%)
  local copies, waits for them, and re-layouts  27.3 us (9%)
  other arithmetic  19.3 us (7%)
  blocking collectives  15.7 us (5%)
  between operations  13.9 us (5%)
    all_gather x1, waiting for transfers between devices, local(): lax.all_gather(narrow_query, 'rows', axis=0, tiled=True)  163 us
    all_gather x1, waiting for transfers between devices, local(): lax.all_gather(narrow_value, 'rows', axis=0, tiled=True)  30.3 us
    unnamed x23, local copies, waits for them, and re-layouts  27.3 us
    all_gather x1, waiting for transfers between devices, local(): lax.all_gather(narrow_key, 'rows', axis=0, tiled=True)  19.7 us
    psum x1, blocking collectives, local(): lax.psum((jnp.sum(jnp.abs(fresh_gained_query), axis=0), jnp.sum(jnp.abs(f...  15.7 us
    reduce_sum x1, other arithmetic, local(): jnp.sum(jnp.abs(fresh_gained_query), axis=0)  10 us
    convert_element_type x1, other arithmetic, local(): (fresh_gained_query / scale_query).astype(jnp.bfloat16)  6.62 us
  transfers between devices with their start and end apart: 3, of which 3 were waited for; matrix products, arithmetic and copies ran while one was open for 3% of the time, Pallas kernels for 0%

commit v1 on v0

v1 whole, which is shorter than its diff:
```python
import functools
import math

import jax
import jax.numpy as jnp
from jax import lax
from jax.experimental import pallas as pl
from jax.experimental.pallas import tpu as pltpu
from jax.sharding import PartitionSpec as P

MESH = pl.DeviceIdType.MESH
CHUNK = 256
STEP_ROWS = 64


def ring_of(chips):
    side = math.isqrt(chips)
    if side * side != chips or side % 2 or side < 2:
        return list(range(chips))
    cycle = [y * side for y in range(side)]
    for k in range(side):
        y = side - 1 - k
        xs = range(1, side) if k % 2 == 0 else range(side - 1, 0, -1)
        cycle += [y * side + x for x in xs]
    return cycle


def pick(table, index):
    out = jnp.int32(table[0])
    for at in range(1, len(table)):
        out = jnp.where(index == at, jnp.int32(table[at]), out)
    return out


def kernel(
    ranks, d_model, plan,
    share_ref, rest_ref, oq, tq, ok, tk, ov, tv,
    sq, sk, sv, cq, ck, cv,
    one_wide, other_wide, narrow_wide, mine_wide, sums_wide,
    one_slim, other_slim, narrow_slim, mine_slim, sums_slim,
    in_sem, stat_send, stat_recv, own_sem, ring_send, ring_recv, twin_send, twin_recv,
):
    me = lax.axis_index("rows")
    chips = ranks // 2
    chip, core = me // 2, me % 2
    cycle = ring_of(chips)
    place = [cycle.index(c) for c in range(chips)]
    spot = pick(place, chip)
    ahead = pick([cycle[(place[c] + 1) % chips] for c in range(chips)], chip)
    behind = pick([cycle[(place[c] - 1) % chips] for c in range(chips)], chip)
    next_dev = (ahead * 2 + core, behind * 2 + core)
    twin = chip * 2 + 1 - core
    rows = oq.shape[0]
    half = rows // 2
    steps = chips // 2
    firsts, others = (oq, ok, ov), (tq, tk, tv)
    outs, scales = (sq, sk, sv), (cq, ck, cv)

    one, other, narrow, mine, sums = {}, {}, {}, {}, {}
    for j, (which, slot, col, width) in enumerate(plan):
        slim = which > 0
        one[j] = (one_slim if slim else one_wide).at[slot]
        other[j] = (other_slim if slim else other_wide).at[slot]
        narrow[j] = (narrow_slim if slim else narrow_wide).at[slot]
        mine[j] = (mine_slim if slim else mine_wide).at[slot]
        for shift in range(1, ranks):
            sums[shift, j] = (sums_slim if slim else sums_wide).at[shift, slot]

    def window(ref, j, first, count):
        which, slot, col, width = plan[j]
        if which > 0:
            return ref.at[pl.ds(first, count)]
        return ref.at[pl.ds(first, count), pl.ds(col, width)]

    def origin(way, step):
        at = lax.rem(spot - step + chips, chips) if way == 0 else lax.rem(spot + step, chips)
        return pick(cycle, at) * 2 + core

    def span(way, step):
        if chips % 2 == 0 and step == steps:
            return way * half, half
        return 0, rows

    loads = []
    for j, (which, slot, col, width) in enumerate(plan):
        pair = []
        for k, (source, held) in enumerate(((firsts, one), (others, other))):
            copy = pltpu.make_async_copy(
                window(source[which], j, 0, rows),
                held[j],
                in_sem.at[k, j],
            )
            copy.start()
            pair.append(copy)
        loads.append(pair)

    barrier = pltpu.get_barrier_semaphore()
    for shift in range(1, ranks):
        pl.semaphore_signal(
            barrier, inc=1, device_id={"rows": lax.rem(me + shift, ranks)}, device_id_type=MESH
        )

    stat_copies = {}
    pending = []

    def tiles(width):
        return [(c, min(128, width - c)) for c in range(0, width, 128)]

    def measure(j):
        which, slot, col, width = plan[j]
        loads[j][0].wait()
        loads[j][1].wait()
        cuts = tiles(width)

        def body(i, accs):
            r = pl.ds(pl.multiple_of(i * STEP_ROWS, STEP_ROWS), STEP_ROWS)
            new = []
            for (c, w), acc in zip(cuts, accs):
                a, b = share_ref[r, pl.ds(0, w)], rest_ref[r, pl.ds(0, w)]
                f = a * one[j][r, pl.ds(c, w)] + b * other[j][r, pl.ds(c, w)]
                one[j][r, pl.ds(c, w)] = f
                new.append(acc + jnp.sum(jnp.abs(f).reshape(STEP_ROWS // 8, 8, w), axis=0))
            return tuple(new)

        accs = lax.fori_loop(
            0, rows // STEP_ROWS, body, tuple(jnp.zeros((8, w), jnp.float32) for _, w in cuts)
        )
        for (c, w), acc in zip(cuts, accs):
            mine[j][:, pl.ds(c, w)] = jnp.sum(acc, axis=0, keepdims=True)

    def share(j):
        if j == 0:
            pl.semaphore_wait(barrier, ranks - 1)
        for shift in range(1, ranks):
            copy = pltpu.make_async_remote_copy(
                src_ref=mine[j],
                dst_ref=sums[shift, j],
                send_sem=stat_send.at[shift, j],
                recv_sem=stat_recv.at[shift, j],
                device_id={"rows": lax.rem(me + shift, ranks)},
                device_id_type=MESH,
            )
            copy.start()
            stat_copies[shift, j] = copy

    def remote(src, dst, send, recv, device):
        copy = pltpu.make_async_remote_copy(
            src_ref=src, dst_ref=dst, send_sem=send, recv_sem=recv,
            device_id={"rows": device}, device_id_type=MESH,
        )
        copy.start()
        return copy

    def block(j, dev, first, count):
        which, slot, col, width = plan[j]
        start = pl.multiple_of(dev * rows + first, half)
        return window(outs[which], j, start, count)

    ring = {}
    twins = {}

    def finish(j):
        which, slot, col, width = plan[j]
        for shift in range(1, ranks):
            stat_copies[shift, j].wait()
        inverses = []
        for c, w in tiles(width):
            total = jnp.zeros((1, w), jnp.float32)
            for owner in range(ranks):
                part = mine[j][:, pl.ds(c, w)]
                for shift in range(1, ranks):
                    sent = sums[shift, j][:, pl.ds(c, w)]
                    part = jnp.where(lax.rem(me - owner + ranks, ranks) == shift, sent, part)
                total = total + part
            scale = total / d_model
            scales[which][:, pl.ds(col + c, w)] = scale
            inverses.append(1.0 / scale)

        def body(i, carry):
            r = pl.ds(pl.multiple_of(i * STEP_ROWS, STEP_ROWS), STEP_ROWS)
            for (c, w), inverse in zip(tiles(width), inverses):
                narrow[j][r, pl.ds(c, w)] = (one[j][r, pl.ds(c, w)] * inverse).astype(jnp.bfloat16)
            return carry

        lax.fori_loop(0, rows // STEP_ROWS, body, 0)

    def send(j):
        which, slot, col, width = plan[j]
        for way in range(2):
            if steps:
                first, count = span(way, 1)
                ring[way, 1, j] = remote(
                    narrow[j].at[pl.ds(first, count)],
                    block(j, me, first, count),
                    ring_send.at[way, 0, j], ring_recv.at[way, 0, j], next_dev[way],
                )
        twins[0, 0, j] = remote(
            narrow[j], block(j, me, 0, rows),
            twin_send.at[0, 0, j], twin_recv.at[0, 0, j], twin,
        )
        copy = pltpu.make_async_copy(
            narrow[j], block(j, me, 0, rows), own_sem.at[j]
        )
        copy.start()
        pending.append(copy)

    count = len(plan)
    measure(0)
    share(0)
    for j in range(count):
        if j + 1 < count:
            measure(j + 1)
            share(j + 1)
        finish(j)
        send(j)

    for step in range(1, steps + 1):
        for j in range(count):
            for way in range(2):
                ring[way, step, j].wait_recv()
                dev = origin(way, step)
                if step < steps:
                    first, n = span(way, step + 1)
                    piece = block(j, dev, first, n)
                    ring[way, step + 1, j] = remote(
                        piece, piece,
                        ring_send.at[way, step, j], ring_recv.at[way, step, j], next_dev[way],
                    )
                first, n = span(way, step)
                piece = block(j, dev, first, n)
                twins[way, step, j] = remote(
                    piece, piece,
                    twin_send.at[way, step, j], twin_recv.at[way, step, j], twin,
                )
    for copy in pending:
        copy.wait()
    for copy in ring.values():
        copy.wait_send()
    for copy in twins.values():
        copy.wait()


def local(ranks, d_model, one_query, other_query, one_key, other_key, one_value, other_value, mix_share, norm_gain):
    rows, q_cols = one_query.shape
    kv_cols = one_key.shape[1]
    width = min(CHUNK, q_cols)
    plan = [(0, col // width, col, width) for col in range(0, q_cols, width)]
    plan += [(1, 0, 0, kv_cols), (2, 1, 0, kv_cols)]
    scratch = []
    for slots, wide in ((q_cols // width, width), (2, kv_cols)):
        scratch += [
            pltpu.VMEM((slots, rows, wide), jnp.float32),
            pltpu.VMEM((slots, rows, wide), jnp.float32),
            pltpu.VMEM((slots, rows, wide), jnp.bfloat16),
            pltpu.VMEM((slots, 1, wide), jnp.float32),
            pltpu.VMEM((ranks, slots, 1, wide), jnp.float32),
        ]
    count = len(plan)
    steps = ranks // 4
    share = jnp.broadcast_to((norm_gain * mix_share)[:, None], (rows, 128))
    rest = jnp.broadcast_to((norm_gain * (1.0 - mix_share))[:, None], (rows, 128))
    whole = ranks * rows
    vmem = pl.BlockSpec(memory_space=pltpu.VMEM)
    hbm = pl.BlockSpec(memory_space=pl.ANY)
    dma = pltpu.SemaphoreType.DMA
    sq, sk, sv, cq, ck, cv = pl.pallas_call(
        functools.partial(kernel, ranks, d_model, plan),
        out_shape=(
            jax.ShapeDtypeStruct((whole, q_cols), jnp.bfloat16),
            jax.ShapeDtypeStruct((whole, kv_cols), jnp.bfloat16),
            jax.ShapeDtypeStruct((whole, kv_cols), jnp.bfloat16),
            jax.ShapeDtypeStruct((1, q_cols), jnp.float32),
            jax.ShapeDtypeStruct((1, kv_cols), jnp.float32),
            jax.ShapeDtypeStruct((1, kv_cols), jnp.float32),
        ),
        in_specs=[vmem, vmem] + [hbm] * 6,
        out_specs=(hbm, hbm, hbm, vmem, vmem, vmem),
        scratch_shapes=scratch
        + [
            dma((2, count)),
            dma((ranks, count)),
            dma((ranks, count)),
            dma((count,)),
            dma((2, max(steps, 1), count)),
            dma((2, max(steps, 1), count)),
            dma((2, steps + 1, count)),
            dma((2, steps + 1, count)),
        ],
        compiler_params=pltpu.CompilerParams(
            collective_id=0, has_side_effects=True, vmem_limit_bytes=50 * 1024 * 1024
        ),
    )(share, rest, one_query, other_query, one_key, other_key, one_value, other_value)
    return sq, sk, sv, cq[0], ck[0], cv[0]


def solution(mesh):
    def body(one_query, *rest):
        ranks = mesh.shape["rows"]
        return local(ranks, ranks * one_query.shape[0], one_query, *rest)

    return jax.shard_map(
        body,
        mesh=mesh,
        in_specs=(P("rows", "cols"),) * 6 + (P("rows"),) * 2,
        out_specs=(P(None, "cols"),) * 3 + (P("cols"),) * 3,
        check_vma=False,
    )
```

time: 289 us -> 202 us (0.70)
  waiting for transfers between devices: 213 us -> 0 us
  Pallas kernels: 0 us -> 167 us
  other arithmetic: 19.3 us -> 0.71 us
  blocking collectives: 15.7 us -> 0 us
  between operations: 13.9 us -> 0.68 us
  local copies, waits for them, and re-layouts: 27.3 us -> 33.6 us
    all_gather x3 -> x0, waiting for transfers between devices: 213 us -> none  [the longest x1 163 us: local(): lax.all_gather(narrow_query, 'rows', axis=0, tiled=True)]
    pallas_call x0 -> x1, Pallas kernels: none -> 167 us  [local(): pl.pallas_call(functools.partial(kernel, ranks, d_model, plan), out_shape...]
    psum x1 -> x0, blocking collectives: 15.7 us -> none  [local(): lax.psum((jnp.sum(jnp.abs(fresh_gained_query), axis=0), jnp.sum(jnp.abs(f...]
    reduce_sum x2 -> x0, other arithmetic: 10.5 us -> none  [the longest x1 10 us: local(): jnp.sum(jnp.abs(fresh_gained_query), axis=0)]
    convert_element_type x3 -> x0, other arithmetic: 8.13 us -> none  [the longest x1 6.62 us: local(): (fresh_gained_query / scale_query).astype(jnp.bfloat16)]
    unnamed x23 -> x16, local copies, waits for them, and re-layouts: 27.3 us -> 33.2 us
  transfers between devices with their start and end apart: 3 -> 0, of which waited for: 3 -> 0; matrix products, arithmetic and copies ran while one was open for 3% -> 0% of each run, Pallas kernels for 0% -> 0%
where the time goes in v1:
time: 202 us
  Pallas kernels  167 us (83%)
  local copies, waits for them, and re-layouts  33.6 us (17%)
    pallas_call x1, Pallas kernels, local(): pl.pallas_call(functools.partial(kernel, ranks, d_model, plan), out_shape...  167 us
    unnamed x16, local copies, waits for them, and re-layouts  33.2 us

profile of v1, /device:TPU:0, one launch (start us, length us, event | category | flops | bytes accessed | tf_op | source)
XLA Modules:
  0.0 201.5 jit_solution(12167391098499488134)
XLA Ops:
  0.6 0.7 subtract_multiply_fusion
  1.3 0.2 broadcast_in_dim.5.rest_ref
  1.5 0.2 broadcast_in_dim.4.share_ref
  1.7 0.0 copy-start
  1.8 1.0 copy-done
  2.8 0.0 copy-start.1
  2.8 1.0 copy-done.1
  3.8 0.0 copy-start.2
  3.8 1.0 copy-done.2
  4.9 0.0 copy-start.3
  4.9 1.0 copy-done.3
  5.9 166.6 %shard_map.127 = (bf16[8192,2048]{1,0:T(8,128)(2,1)}, bf16[8192,128]{1,0:T(8,128)(2,1)}, bf16[8192,128]{1,0:T(8,128)(2,1)}, f32[1,2048]{1,0:T(1,128)S(1)}, f32[1,128]{1,0:T(1,128)S(1)}, /*index=5*/f32[1,128]{1,0:T(1,128)S(1)}) custom-call(f32[1024,128]{1,0:T(8,128)S(1)} %broadcast_in_dim.4.share_ref, f32[1024,128]{1,0:T(8,128)S(1)} %broadcast_in_dim.5.rest_ref, ...), custom_call_target="tpu_custom_call" | custom-call | tf_op jit(solution)/shard_map/pallas_call | solution.py:266
  172.5 0.0 copy-start.4
  172.5 23.0 %copy.20 = bf16[8192,2048]{1,0:T(8,128)(2,1)} copy(bf16[8192,2048]{1,0:T(8,128)(2,1)} %get-tuple-element.26) | data formatting | bytes 67108864
  195.5 3.0 %copy.21 = bf16[8192,128]{1,0:T(8,128)(2,1)} copy(bf16[8192,128]{1,0:T(8,128)(2,1)} %get-tuple-element.27) | data formatting | bytes 4194304
  198.6 0.0 copy-done.4
  198.6 1.3 copy.22
  199.9 0.6 copy.23
  200.5 0.5 copy.24
  201.0 0.5 copy.25
Async XLA Ops:
  1.7 1.0 copy-start
  2.8 1.0 copy-start.1
  3.8 1.0 copy-start.2
  4.9 1.0 copy-start.3
  172.5 26.1 %copy-start.4 = (bf16[8192,128]{1,0:T(8,128)(2,1)S(1)}, bf16[8192,128]{1,0:T(8,128)(2,1)}, u32[]{:S(2)}) copy-start(bf16[8192,128]{1,0:T(8,128)(2,1)} %get-tuple-element.28) | copy-start | bytes 6291460
